TPU v7x, 32 devices: a whole 2x2x4 slice. The times are simulated.
32 devices in a mesh: dp: 16 (over z, y, core), space: 2 (over x).
Axes of the slice: x: 2, y: 2, z: 4, core: 2. Of those that a mesh axis runs over, the one named last changes fastest.
Arguments:
- feature_map: bfloat16 [16, 24, 84, 256], P('dp', 'space'), may hold values from -6 to 6
- proposals: int32 [16, 128, 4], P('dp'), may hold values from 0 to 84, as said below
- hidden_weight: bfloat16 [12544, 512], P(None, 'space'), may hold values from -0.0546875 to 0.0546875
- output_weight: bfloat16 [512, 512], P('space'), may hold values from -0.25 to 0.25
- upstream: bfloat16 [16, 128, 512], P('dp'), may hold values from -6 to 6
Outputs:
- hidden_weight_grad: float32 [12544, 512], P('dp', 'space')
- output_weight_grad: float32 [512, 512], P('space')
- feature_grad: float32 [16, 24, 84, 256], P('dp', 'space')
Inputs may be any that keep to these rules, and one draw needn't show every extreme that they name: `proposals`: each row holds top, left, bottom, right with top < bottom <= 24 and left < right <= 84.
All inputs are finite; a program needn't handle non-finite values.
Results may differ from a plain program's by a relative error of at most 0.012.
Values may be sent and summed in bfloat16 or wider, within the bound.
No kernel may reach another device: no remote copies, remote signals or barrier semaphores. Data moves between devices by JAX's collectives and lax.ppermute only.
A program may use at most 128 MiB of HBM per device.

v0:
```python
import jax
import jax.numpy as jnp
from jax import lax
from jax.sharding import PartitionSpec as P

POOL = 7


def axis_weights(low_edge, high_edge, grid_points):
    edge_start = low_edge.astype(jnp.float32)
    bin_size = (high_edge - low_edge).astype(jnp.float32) / POOL
    bin_index = jnp.arange(POOL).astype(jnp.float32)
    offsets = jnp.array([0.25, 0.75], jnp.float32)
    sample_points = (
        edge_start[:, None, None]
        + (bin_index[None, :, None] + offsets[None, None, :]) * bin_size[:, None, None]
        - 0.5
    )
    weights = jnp.maximum(
        0.0, 1.0 - jnp.abs(sample_points[..., None] - grid_points[None, None, None, :])
    )
    return jnp.mean(weights, axis=2)


def activate(values):
    return jax.nn.gelu(values, approximate=True)


def gelu_grad(values, incoming):
    return jax.vjp(activate, values)[1](incoming)[0]


def block_shape(proposal_count):
    block_size = 32
    return (block_size, proposal_count // block_size)


def crop_rows(own_map, row_weight, col_weight):
    height_cells, width_cells, channels = own_map.shape
    proposal_count = row_weight.shape[0]
    block_size, block_count = block_shape(proposal_count)
    flattened = jnp.transpose(own_map, (1, 0, 2)).reshape(width_cells, height_cells * channels)

    def per_block(blocks):
        row_part, col_part = blocks
        across = jnp.dot(
            col_part.reshape(block_size * POOL, width_cells),
            flattened,
            preferred_element_type=jnp.float32,
        )
        across = across.reshape(block_size, POOL, height_cells, channels)
        return jnp.einsum("riy,rjyc->rijc", row_part, across, precision=lax.Precision.HIGHEST)

    pooled = lax.map(
        per_block,
        (
            row_weight.reshape(block_count, block_size, POOL, height_cells),
            col_weight.reshape(block_count, block_size, POOL, width_cells),
        ),
    )
    return pooled.reshape(proposal_count, POOL * POOL * channels)


def crop_back(grad_pooled, row_weight, col_weight, channels):
    proposal_count, _, height_cells = row_weight.shape
    width_cells = col_weight.shape[2]
    block_size, block_count = block_shape(proposal_count)

    def per_block(running, blocks):
        row_part, col_part, grad_part = blocks
        grad_block = grad_part.reshape(block_size, POOL, POOL, channels)
        spread = jnp.einsum("riy,rijc->rjyc", row_part, grad_block, precision=lax.Precision.HIGHEST)
        added = lax.dot_general(
            col_part.astype(jnp.float32).reshape(block_size * POOL, width_cells),
            spread.reshape(block_size * POOL, height_cells * channels),
            (((0,), (0,)), ((), ())),
            precision=lax.Precision.HIGHEST,
            preferred_element_type=jnp.float32,
        )
        return (running + added, None)

    start = jnp.zeros((width_cells, height_cells * channels), jnp.float32)
    blocks = (
        row_weight.reshape(block_count, block_size, POOL, height_cells),
        col_weight.reshape(block_count, block_size, POOL, width_cells),
        grad_pooled.reshape(block_count, block_size, grad_pooled.shape[1]),
    )
    total, _ = lax.scan(per_block, start, blocks)
    return jnp.transpose(total.reshape(width_cells, height_cells, channels), (1, 0, 2))


def on_device(feature_map, proposals, hidden_weight, output_weight, upstream):
    own_map = feature_map[0]
    corners = proposals[0]
    own_height = own_map.shape[0]
    map_width = own_map.shape[1]
    channels = own_map.shape[2]
    row_offset = lax.axis_index("space") * own_height
    local_grid = (row_offset + jnp.arange(own_height, dtype=jnp.int32)).astype(jnp.float32)
    row_weight = axis_weights(corners[:, 0], corners[:, 2], local_grid)
    col_weight = axis_weights(
        corners[:, 1], corners[:, 3], jnp.arange(map_width, dtype=jnp.int32).astype(jnp.float32)
    ).astype(jnp.bfloat16)
    full_grid = jnp.arange(own_height * lax.axis_size("space"), dtype=jnp.int32).astype(jnp.float32)
    full_weight = axis_weights(corners[:, 0], corners[:, 2], full_grid)
    whole_map = lax.all_gather(own_map, "space", axis=0, tiled=True)
    pooled = crop_rows(whole_map, full_weight, col_weight).astype(jnp.bfloat16)
    pre_hidden = jnp.dot(pooled, hidden_weight, preferred_element_type=jnp.float32)
    hidden = activate(pre_hidden).astype(jnp.bfloat16)
    pre_output = lax.psum(
        jnp.dot(hidden, output_weight, preferred_element_type=jnp.float32).astype(jnp.bfloat16),
        "space",
    ).astype(jnp.float32)
    output_delta = gelu_grad(pre_output, upstream[0].astype(jnp.float32)).astype(jnp.bfloat16)
    step_second = lax.dot_general(
        hidden, output_delta, (((0,), (0,)), ((), ())), preferred_element_type=jnp.float32
    )
    second_total = lax.psum(step_second, "dp")
    hidden_back = lax.dot_general(
        output_delta, output_weight, (((1,), (1,)), ((), ())), preferred_element_type=jnp.float32
    )
    hidden_delta = gelu_grad(pre_hidden, hidden_back).astype(jnp.bfloat16)
    column_rows = lax.all_to_all(pooled, "dp", split_axis=1, concat_axis=0, tiled=True)
    delta_rows = lax.all_gather(hidden_delta, "dp", axis=0, tiled=True)
    first_total = lax.dot_general(
        column_rows, delta_rows, (((0,), (0,)), ((), ())), preferred_element_type=jnp.float32
    )
    partial_grad = lax.dot_general(
        hidden_delta, hidden_weight, (((1,), (1,)), ((), ())), preferred_element_type=jnp.float32
    )
    grad_share = lax.psum_scatter(
        partial_grad.astype(jnp.bfloat16), "space", scatter_dimension=0, tiled=True
    ).astype(jnp.float32)
    pooled_grad = lax.all_gather(
        grad_share.astype(jnp.bfloat16), "space", axis=0, tiled=True
    ).astype(grad_share.dtype)
    map_grad = crop_back(pooled_grad, row_weight, col_weight, channels)
    return (first_total, second_total, map_grad[None])


def solution(mesh):
    placed = (
        P("dp", "space", None, None),
        P("dp", None, None),
        P(None, "space"),
        P("space", None),
        P("dp", None, None),
    )
    return jax.shard_map(
        on_device,
        mesh=mesh,
        in_specs=placed,
        out_specs=(P("dp", "space"), P("space", None), P("dp", "space", None, None)),
        check_vma=False,
    )
```

profile of v0, /device:TPU:0, one launch (start us, length us, event | category | flops | bytes accessed | tf_op | source)
XLA Modules:
  0.0 361.1 jit_solution(6747203176717695255)
XLA Ops:
  11.3 16.2 %all-gather = bf16[1,24,84,256]{3,2,0,1:T(8,128)(2,1)S(1)} all-gather(bf16[1,12,84,256]{3,2,0,1:T(8,128)(2,1)} %bitcast.120), channel_id=2, replica_groups=mesh['dp'=16,'space'=2] {'space'}, dimensions={1}, use_global_device_ids=true | all-gather | bytes 1548288 | tf_op jit(solution)/shard_map/all_gather | solution.py:106
  28.0 34.6 %while.21 = (s32[]{:T(128)}, bf16[4,32,7,7,256]{4,2,3,1,0:T(8,128)(2,1)}, f32[4,32,7,24]{3,2,1,0:T(8,128)S(1)}, bf16[4,32,7,84]{3,1,0,2:T(8,128)(2,1)S(1)}, bf16[84,6144]{1,0:T(8,128)(2,1)S(1)}, /*index=5*/s32[]{:T(128)}) while((s32[]{:T(128)}, bf16[4,32,7,7,256]{4,2,3,1,0:T(8,128)(2,1)}, f32[4,32,7,24]{3,2,1,0:T(8,128)S(1)}, ...), condition=%wide.region_3.4_spmd, body=%wide.region_2.0_spmd.sunk | while | flops 346816512 | bytes 18293832 | solution.py:54
  29.2 7.5 %bitcast_dynamic-update-slice_fusion.2 = bf16[4,32,7,7,256]{4,2,3,1,0:T(8,128)(2,1)} fusion(bf16[4,32,7,7,256]{4,2,3,1,0:T(8,128)(2,1)} %get-tuple-element.230, s32[]{:T(128)} %get-tuple-element.229, f32[32,7,24,256]{3,0,2,1:T(8,128)S(1)} %fusion.66, f32[4,32,7,24]{3,2,1,0:T(8,128)S(1)} %get-tuple-element.237), kind=kOutput, calls=%fused_computation.2.clone.1 | convolution fusion | flops 115605504 | bytes 7472128 | tf_op jit(solution)/shard_map/while/body/eval_jaxpr/riy,rjyc->rijc/dot_general | solution.py:52
  37.8 7.5 %bitcast_dynamic-update-slice_fusion.2 = bf16[4,32,7,7,256]{4,2,3,1,0:T(8,128)(2,1)} fusion(bf16[4,32,7,7,256]{4,2,3,1,0:T(8,128)(2,1)} %get-tuple-element.230, s32[]{:T(128)} %get-tuple-element.229, f32[32,7,24,256]{3,0,2,1:T(8,128)S(1)} %fusion.66, f32[4,32,7,24]{3,2,1,0:T(8,128)S(1)} %get-tuple-element.237), kind=kOutput, calls=%fused_computation.2.clone.1 | convolution fusion | flops 115605504 | bytes 7472128 | tf_op jit(solution)/shard_map/while/body/eval_jaxpr/riy,rjyc->rijc/dot_general | solution.py:52
  46.5 7.5 %bitcast_dynamic-update-slice_fusion.2 = bf16[4,32,7,7,256]{4,2,3,1,0:T(8,128)(2,1)} fusion(bf16[4,32,7,7,256]{4,2,3,1,0:T(8,128)(2,1)} %get-tuple-element.230, s32[]{:T(128)} %get-tuple-element.229, f32[32,7,24,256]{3,0,2,1:T(8,128)S(1)} %fusion.66, f32[4,32,7,24]{3,2,1,0:T(8,128)S(1)} %get-tuple-element.237), kind=kOutput, calls=%fused_computation.2.clone.1 | convolution fusion | flops 115605504 | bytes 7472128 | tf_op jit(solution)/shard_map/while/body/eval_jaxpr/riy,rjyc->rijc/dot_general | solution.py:52
  55.2 7.5 %bitcast_dynamic-update-slice_fusion.2 = bf16[4,32,7,7,256]{4,2,3,1,0:T(8,128)(2,1)} fusion(bf16[4,32,7,7,256]{4,2,3,1,0:T(8,128)(2,1)} %get-tuple-element.230, s32[]{:T(128)} %get-tuple-element.229, f32[32,7,24,256]{3,0,2,1:T(8,128)S(1)} %fusion.66, f32[4,32,7,24]{3,2,1,0:T(8,128)S(1)} %get-tuple-element.237), kind=kOutput, calls=%fused_computation.2.clone.1 | convolution fusion | flops 115605504 | bytes 7472128 | tf_op jit(solution)/shard_map/while/body/eval_jaxpr/riy,rjyc->rijc/dot_general | solution.py:52
  62.6 5.1 %copy.77 = bf16[4,32,7,7,256]{4,3,2,1,0:T(8,128)(2,1)} copy(bf16[4,32,7,7,256]{4,2,3,1,0:T(8,128)(2,1)} %get-tuple-element.57) | data formatting | bytes 6422528 | tf_op jit(solution)/shard_map/convert_element_type | solution.py:107
  67.8 5.6 %convert_element_type.132 = bf16[128,12544]{1,0:T(8,128)(2,1)S(1)} reshape(bf16[4,32,7,7,256]{4,3,2,1,0:T(8,128)(2,1)} %copy.77) | data formatting | bytes 6422528 | tf_op jit(solution)/shard_map/convert_element_type | solution.py:107
  73.4 3.8 %fusion.39 = f32[128,256]{1,0:T(8,128)S(1)} fusion(bf16[128,12544]{1,0:T(8,128)(2,1)S(1)} %convert_element_type.132, bf16[12544,256]{1,0:T(8,128)(2,1)} %param.14), kind=kOutput, calls=%fused_computation.69 | convolution fusion | flops 822083584 | bytes 9764864 | tf_op jit(solution)/shard_map/dot_general | solution.py:108
  79.0 22.9 %all-reduce.3.cloned.1.call-done = bf16[128,512]{1,0:T(8,128)(2,1)} async-done(((bf16[128,512]{1,0:T(8,128)(2,1)}), bf16[128,512]{1,0:T(8,128)(2,1)}) %all-reduce.3.cloned.1.call-update) | async-done | bytes 131088 | tf_op jit(solution)/shard_map/psum | solution.py:110
  104.9 6.8 %convolution_convert_fusion = bf16[128,12544]{1,0:T(8,128)(2,1)} fusion(bf16[128,256]{1,0:T(8,128)(2,1)S(1)} %fusion.37, bf16[12544,256]{1,0:T(8,128)(2,1)} %param.14), kind=kOutput, calls=%fused_computation.21 | convolution fusion | flops 823689216 | bytes 9699328 | tf_op jit(solution)/shard_map/dot_general | solution.py:128
  111.7 9.3 %convert_element_type.129 = bf16[128,16,784]{2,1,0:T(8,128)(2,1)} reshape(bf16[4,32,7,7,256]{4,3,2,1,0:T(8,128)(2,1)} %copy.77) | data formatting | bytes 6422528 | tf_op jit(solution)/shard_map/convert_element_type | solution.py:107
  121.0 6.2 %copy.78 = bf16[128,16,784]{0,2,1:T(8,128)(2,1)} copy(bf16[128,16,784]{2,1,0:T(8,128)(2,1)} %convert_element_type.129) | data formatting | bytes 6422528 | tf_op jit(solution)/shard_map/convert_element_type | solution.py:107
  127.2 5.8 %all-to-all-start = ((bf16[128,16,784]{0,2,1:T(8,128)(2,1)}), bf16[128,16,784]{0,2,1:T(8,128)(2,1)S(1)}, u32[]{:S(2)}, u32[]{:S(2)}) async-start(bf16[128,16,784]{0,2,1:T(8,128)(2,1)} %copy.78), calls=%async_computation | async-start | bytes 6422528 | tf_op jit(solution)/shard_map/all_to_all | solution.py:123
  133.8 22.2 %reduce-scatter.2.cloned.1.call-done = bf16[64,12544]{1,0:T(8,128)(2,1)} async-done(((bf16[128,12544]{1,0:T(8,128)(2,1)}), bf16[64,12544]{1,0:T(8,128)(2,1)}) %reduce-scatter.2.cloned.1.call-update) | async-done | bytes 1605648 | tf_op jit(solution)/shard_map/reduce_scatter | solution.py:131
  160.2 50.5 %all-gather.4.cloned.1.call-done = bf16[2048,256]{1,0:T(8,128)(2,1)} async-done(((bf16[128,256]{1,0:T(8,128)(2,1)}), bf16[2048,256]{1,0:T(8,128)(2,1)}) %all-gather.4.cloned.1.call-update) | async-done | bytes 1048592 | tf_op jit(solution)/shard_map/all_gather | solution.py:124
  210.8 3.1 fusion.18
  213.9 44.3 %all-gather.6.cloned.1.call-done = bf16[128,12544]{1,0:T(8,128)(2,1)} async-done(((bf16[64,12544]{1,0:T(8,128)(2,1)}), bf16[128,12544]{1,0:T(8,128)(2,1)}) %all-gather.6.cloned.1.call-update) | async-done | bytes 3211280 | tf_op jit(solution)/shard_map/all_gather | solution.py:134
  258.2 5.1 %convert.3 = f32[4,32,12544]{2,1,0:T(8,128)} convert(bf16[4,32,12544]{2,1,0:T(8,128)(2,1)} %bitcast.115) | non-fusion elementwise | flops 1605632 | bytes 9633792 | tf_op jit(solution)/shard_map/reshape | solution.py:86
  263.3 51.9 %while.22 = (s32[]{:T(128)}, f32[84,3072]{1,0:T(8,128)}, bf16[4,32,7,84]{3,2,1,0:T(8,128)(2,1)}, f32[4,32,12544]{2,1,0:T(8,128)}, f32[4,32,7,12]{3,2,1,0:T(8,128)}, /*index=5*/s32[]{:T(128)}, s32[]{:T(128)}) while((s32[]{:T(128)}, f32[84,3072]{1,0:T(8,128)}, bf16[4,32,7,84]{3,2,1,0:T(8,128)(2,1)}, f32[4,32,12544]{2,1,0:T(8,128)}, ...), condition=%wide.region_9.10_spmd.clone, body=%wide.region_8.9_spmd.clone.sunk | while | flops 751951872 | bytes 21422432 | solution.py:88
  265.3 4.5 %fusion.71 = f32[32,7,256,12]{2,3,1,0:T(8,128)S(1)} fusion(f32[32,7,7,256]{3,2,1,0:T(8,128)S(1)} %reshape.239, f32[4,32,7,12]{3,2,1,0:T(8,128)} %get-tuple-element.259, s32[]{:T(128)} %get-tuple-element.248), kind=kOutput, calls=%fused_computation.14.clone.1 | convolution fusion | flops 57802752 | bytes 4489728 | tf_op jit(solution)/shard_map/while/body/eval_jaxpr/riy,rijc->rjyc/dot_general | solution.py:72
  269.8 2.4 copy.120
  277.3 4.5 %fusion.71 = f32[32,7,256,12]{2,3,1,0:T(8,128)S(1)} fusion(f32[32,7,7,256]{3,2,1,0:T(8,128)S(1)} %reshape.239, f32[4,32,7,12]{3,2,1,0:T(8,128)} %get-tuple-element.259, s32[]{:T(128)} %get-tuple-element.248), kind=kOutput, calls=%fused_computation.14.clone.1 | convolution fusion | flops 57802752 | bytes 4489728 | tf_op jit(solution)/shard_map/while/body/eval_jaxpr/riy,rijc->rjyc/dot_general | solution.py:72
  281.8 2.4 copy.120
  285.1 3.5 convolution_add_fusion.2
  290.6 4.5 %fusion.71 = f32[32,7,256,12]{2,3,1,0:T(8,128)S(1)} fusion(f32[32,7,7,256]{3,2,1,0:T(8,128)S(1)} %reshape.239, f32[4,32,7,12]{3,2,1,0:T(8,128)} %get-tuple-element.259, s32[]{:T(128)} %get-tuple-element.248), kind=kOutput, calls=%fused_computation.14.clone.1 | convolution fusion | flops 57802752 | bytes 4489728 | tf_op jit(solution)/shard_map/while/body/eval_jaxpr/riy,rijc->rjyc/dot_general | solution.py:72
  295.1 2.4 copy.120
  298.4 3.5 convolution_add_fusion.2
  303.9 4.5 %fusion.71 = f32[32,7,256,12]{2,3,1,0:T(8,128)S(1)} fusion(f32[32,7,7,256]{3,2,1,0:T(8,128)S(1)} %reshape.239, f32[4,32,7,12]{3,2,1,0:T(8,128)} %get-tuple-element.259, s32[]{:T(128)} %get-tuple-element.248), kind=kOutput, calls=%fused_computation.14.clone.1 | convolution fusion | flops 57802752 | bytes 4489728 | tf_op jit(solution)/shard_map/while/body/eval_jaxpr/riy,rijc->rjyc/dot_general | solution.py:72
  308.4 2.4 copy.120
  311.7 3.5 convolution_add_fusion.2
  318.8 33.9 %all-reduce.5.cloned.1.call-done = f32[256,512]{1,0:T(8,128)} async-done(((f32[256,512]{1,0:T(8,128)}), f32[256,512]{1,0:T(8,128)}) %all-reduce.5.cloned.1.call-update) | async-done | bytes 524304 | tf_op jit(solution)/shard_map/psum | solution.py:118
  (86 shorter events, 38.1 us)
Async XLA Ops:
  7.2 70.7 %copy-start = (bf16[256,512]{1,0:T(8,128)(2,1)S(1)}, bf16[256,512]{1,0:T(8,128)(2,1)}, u32[]{:S(2)}) copy-start(bf16[256,512]{1,0:T(8,128)(2,1)} %param.15) | copy-start | bytes 786436
  7.2 94.7 %all-reduce.3.cloned.1.call-start = ((), (), s32[]{:S(2)}) async-start(), calls=%async_computation.2 | async-start | bytes 262144 | tf_op jit(solution)/shard_map/psum | solution.py:110
  10.7 17.0 %copy-start.2 = (bf16[128,7,84]{0,2,1:T(8,128)(2,1)}, bf16[128,7,84]{0,2,1:T(8,128)(2,1)S(1)}, u32[]{:S(2)}) copy-start(bf16[128,7,84]{0,2,1:T(8,128)(2,1)S(1)} %multiply_convert_fusion) | copy-start | bytes 451588
  77.2 0.7 copy-start.4
  78.7 77.3 %reduce-scatter.2.cloned.1.call-start = ((), (), s32[]{:S(2)}) async-start(), calls=%async_computation.5 | async-start | bytes 4816896 | tf_op jit(solution)/shard_map/reduce_scatter | solution.py:131
  103.0 0.6 copy-start.6
  104.8 6.8 %copy-start.7 = (bf16[128,256]{1,0:T(8,128)(2,1)}, bf16[128,256]{1,0:T(8,128)(2,1)S(1)}, u32[]{:S(2)}) copy-start(bf16[128,256]{1,0:T(8,128)(2,1)S(1)} %fusion.37) | copy-start | bytes 196612
  127.2 28.8 %copy-start.3 = (bf16[128,7,84]{0,2,1:T(8,128)(2,1)S(1)}, bf16[128,7,84]{0,2,1:T(8,128)(2,1)}, u32[]{:S(2)}) copy-start(bf16[128,7,84]{0,2,1:T(8,128)(2,1)} %copy-done.2) | copy-start | bytes 451588
  127.2 31.0 %copy-start.5 = (f32[128,256]{1,0:T(8,128)S(1)}, f32[128,256]{1,0:T(8,128)}, u32[]{:S(2)}) copy-start(f32[128,256]{1,0:T(8,128)} %copy-done.4) | copy-start | bytes 393220
  127.2 83.6 %all-to-all-start = ((bf16[128,16,784]{0,2,1:T(8,128)(2,1)}), bf16[128,16,784]{0,2,1:T(8,128)(2,1)S(1)}, u32[]{:S(2)}, u32[]{:S(2)}) async-start(bf16[128,16,784]{0,2,1:T(8,128)(2,1)} %copy.78), calls=%async_computation | async-start | bytes 6422528 | tf_op jit(solution)/shard_map/all_to_all | solution.py:123
  133.0 77.8 %all-gather.4.cloned.1.call-start = ((), (), s32[]{:S(2)}) async-start(), calls=%async_computation.3 | async-start | bytes 1114112 | tf_op jit(solution)/shard_map/all_gather | solution.py:124
  133.7 124.4 %all-gather.6.cloned.1.call-start = ((), (), s32[]{:S(2)}) async-start(), calls=%async_computation.6 | async-start | bytes 4816896 | tf_op jit(solution)/shard_map/all_gather | solution.py:134
  156.0 196.7 %all-reduce.5.cloned.1.call-start = ((), (), s32[]{:S(2)}) async-start(), calls=%async_computation.4 | async-start | bytes 1048576 | tf_op jit(solution)/shard_map/psum | solution.py:118
  315.2 39.4 %copy-start.1 = (bf16[256,512]{1,0:T(8,128)(2,1)S(1)}, bf16[256,512]{1,0:T(8,128)(2,1)}, u32[]{:S(2)}) copy-start(bf16[256,512]{1,0:T(8,128)(2,1)} %param.15) | copy-start | bytes 786436
Sparse Core Ops, SparseCore 0:
  78.9 22.9 all-reduce.2
  111.8 44.1 reduce-scatter.1
  158.2 52.5 all-gather.3
  212.2 45.9 all-gather.5
  262.0 90.6 all-reduce.4
where the time goes:
time: 363 us; the launch traced here: 361 us
  waiting for transfers between devices  175 us (48%)
  matrix products  81.6 us (22%)
  local copies, waits for them, and re-layouts  58.4 us (16%)
  blocking collectives  16.2 us (4%)
  between operations  14 us (4%)
  other arithmetic  10.1 us (3%)
  starting transfers between devices  6.13 us (2%)
    all_gather x1, waiting for transfers between devices, on_device(): delta_rows = lax.all_gather(hidden_delta, 'dp', axis=0, tiled=True)  50.5 us
    all_gather x1, waiting for transfers between devices, on_device(): lax.all_gather(grad_share.astype(jnp.bfloat16), 'space', axis=0, tiled=True)  44.3 us
    psum x1, waiting for transfers between devices, on_device(): second_total = lax.psum(step_second, 'dp')  33.9 us
    dot_general x4, matrix products, per_block(): jnp.einsum('riy,rjyc->rijc', row_part, across, precision=lax.Precision.HI...  29.9 us
    convert_element_type x4, local copies, waits for them, and re-layouts, on_device(): pooled = crop_rows(whole_map, full_weight, col_weight).astype(jnp.bfloat16)  26.3 us
    psum x1, waiting for transfers between devices, on_device(): lax.psum(jnp.dot(hidden, output_weight, preferred_element_type=jnp.float3...  22.9 us
    reduce_scatter x1, waiting for transfers between devices, on_device(): lax.psum_scatter(partial_grad.astype(jnp.bfloat16), 'space', scatter_dime...  22.2 us
    dot_general x4, matrix products, per_block(): jnp.einsum('riy,rijc->rjyc', row_part, grad_block, precision=lax.Precisio...  17.9 us
  transfers between devices with their start and end apart: 6, of which 5 were waited for; matrix products, arithmetic and copies ran while one was open for 23% of the time, Pallas kernels for 0%

commit v1 on v0

--- a/solution.py
+++ b/solution.py
@@ -115,7 +115,11 @@
     step_second = lax.dot_general(
         hidden, output_delta, (((0,), (0,)), ((), ())), preferred_element_type=jnp.float32
     )
-    second_total = lax.psum(step_second, "dp")
+    second_total = step_second
+    for hop in (1, 2, 4, 8):
+        second_total = second_total + lax.ppermute(
+            second_total, "dp", [(dev, dev ^ hop) for dev in range(16)]
+        )
     hidden_back = lax.dot_general(
         output_delta, output_weight, (((1,), (1,)), ((), ())), preferred_element_type=jnp.float32
     )

time: 363 us -> 330 us (0.909)
  waiting for transfers between devices: 175 us -> 133 us
  starting transfers between devices: 6.13 us -> 15 us
    ppermute x0 -> x4, waiting for transfers between devices: none -> 69.7 us  [on_device(): lax.ppermute(second_total, 'dp', [(dev, dev ^ hop) for dev in range(16)])]
    all_gather x1, waiting for transfers between devices: 50.5 us -> 0.01 us  [on_device(): delta_rows = lax.all_gather(hidden_delta, 'dp', axis=0, tiled=True)]
    psum x1 -> x0, waiting for transfers between devices: 33.9 us -> none  [on_device(): second_total = lax.psum(step_second, 'dp')]
    all_gather x1, waiting for transfers between devices: 44.3 us -> 17 us  [on_device(): lax.all_gather(grad_share.astype(jnp.bfloat16), 'space', axis=0, tiled=True)]
    ppermute x0 -> x4, starting transfers between devices: none -> 8.9 us  [on_device(): lax.ppermute(second_total, 'dp', [(dev, dev ^ hop) for dev in range(16)])]
  transfers between devices with their start and end apart: 6 -> 9, of which waited for: 5 -> 7; matrix products, arithmetic and copies ran while one was open for 23% -> 8% of each run, Pallas kernels for 0% -> 0%
where the time goes in v1:
time: 330 us; the launch traced here: 329 us
  waiting for transfers between devices  133 us (40%)
  matrix products  80.9 us (25%)
  local copies, waits for them, and re-layouts  56.5 us (17%)
  blocking collectives  16.2 us (5%)
  starting transfers between devices  15 us (5%)
  between operations  14 us (4%)
  other arithmetic  13.2 us (4%)
    ppermute x4, waiting for transfers between devices, on_device(): lax.ppermute(second_total, 'dp', [(dev, dev ^ hop) for dev in range(16)])  69.7 us
    dot_general x4, matrix products, per_block(): jnp.einsum('riy,rjyc->rijc', row_part, across, precision=lax.Precision.HI...  29.9 us
    convert_element_type x4, local copies, waits for them, and re-layouts, on_device(): pooled = crop_rows(whole_map, full_weight, col_weight).astype(jnp.bfloat16)  26.3 us
    psum x1, waiting for transfers between devices, on_device(): lax.psum(jnp.dot(hidden, output_weight, preferred_element_type=jnp.float3...  22.9 us
    reduce_scatter x1, waiting for transfers between devices, on_device(): lax.psum_scatter(partial_grad.astype(jnp.bfloat16), 'space', scatter_dime...  22.2 us
    dot_general x4, matrix products, per_block(): jnp.einsum('riy,rijc->rjyc', row_part, grad_block, precision=lax.Precisio...  17.9 us
    all_gather x1, waiting for transfers between devices, on_device(): lax.all_gather(grad_share.astype(jnp.bfloat16), 'space', axis=0, tiled=True)  17 us
    all_gather x1, blocking collectives, on_device(): whole_map = lax.all_gather(own_map, 'space', axis=0, tiled=True)  16.2 us
  transfers between devices with their start and end apart: 9, of which 7 were waited for; matrix products, arithmetic and copies ran while one was open for 8% of the time, Pallas kernels for 0%

profile of v1, /device:TPU:0, one launch (start us, length us, event | category | flops | bytes accessed | tf_op | source)
XLA Modules:
  0.0 328.5 jit_solution(246690148872526134)
XLA Ops:
  11.3 16.2 %all-gather = bf16[1,24,84,256]{3,2,0,1:T(8,128)(2,1)S(1)} all-gather(bf16[1,12,84,256]{3,2,0,1:T(8,128)(2,1)} %bitcast.120), channel_id=2, replica_groups=mesh['dp'=16,'space'=2] {'space'}, dimensions={1}, use_global_device_ids=true | all-gather | bytes 1548288 | tf_op jit(solution)/shard_map/all_gather | solution.py:106
  28.0 34.6 %while.21 = (s32[]{:T(128)}, bf16[4,32,7,7,256]{4,2,3,1,0:T(8,128)(2,1)}, f32[4,32,7,24]{3,2,1,0:T(8,128)S(1)}, bf16[4,32,7,84]{3,1,0,2:T(8,128)(2,1)S(1)}, bf16[84,6144]{1,0:T(8,128)(2,1)S(1)}, /*index=5*/s32[]{:T(128)}) while((s32[]{:T(128)}, bf16[4,32,7,7,256]{4,2,3,1,0:T(8,128)(2,1)}, f32[4,32,7,24]{3,2,1,0:T(8,128)S(1)}, ...), condition=%wide.region_3.4_spmd, body=%wide.region_2.0_spmd.sunk | while | flops 346816512 | bytes 18293832 | solution.py:54
  29.2 7.5 %bitcast_dynamic-update-slice_fusion.2 = bf16[4,32,7,7,256]{4,2,3,1,0:T(8,128)(2,1)} fusion(bf16[4,32,7,7,256]{4,2,3,1,0:T(8,128)(2,1)} %get-tuple-element.230, s32[]{:T(128)} %get-tuple-element.229, f32[32,7,24,256]{3,0,2,1:T(8,128)S(1)} %fusion.66, f32[4,32,7,24]{3,2,1,0:T(8,128)S(1)} %get-tuple-element.237), kind=kOutput, calls=%fused_computation.2.clone.1 | convolution fusion | flops 115605504 | bytes 7472128 | tf_op jit(solution)/shard_map/while/body/eval_jaxpr/riy,rjyc->rijc/dot_general | solution.py:52
  37.9 7.5 %bitcast_dynamic-update-slice_fusion.2 = bf16[4,32,7,7,256]{4,2,3,1,0:T(8,128)(2,1)} fusion(bf16[4,32,7,7,256]{4,2,3,1,0:T(8,128)(2,1)} %get-tuple-element.230, s32[]{:T(128)} %get-tuple-element.229, f32[32,7,24,256]{3,0,2,1:T(8,128)S(1)} %fusion.66, f32[4,32,7,24]{3,2,1,0:T(8,128)S(1)} %get-tuple-element.237), kind=kOutput, calls=%fused_computation.2.clone.1 | convolution fusion | flops 115605504 | bytes 7472128 | tf_op jit(solution)/shard_map/while/body/eval_jaxpr/riy,rjyc->rijc/dot_general | solution.py:52
  46.5 7.5 %bitcast_dynamic-update-slice_fusion.2 = bf16[4,32,7,7,256]{4,2,3,1,0:T(8,128)(2,1)} fusion(bf16[4,32,7,7,256]{4,2,3,1,0:T(8,128)(2,1)} %get-tuple-element.230, s32[]{:T(128)} %get-tuple-element.229, f32[32,7,24,256]{3,0,2,1:T(8,128)S(1)} %fusion.66, f32[4,32,7,24]{3,2,1,0:T(8,128)S(1)} %get-tuple-element.237), kind=kOutput, calls=%fused_computation.2.clone.1 | convolution fusion | flops 115605504 | bytes 7472128 | tf_op jit(solution)/shard_map/while/body/eval_jaxpr/riy,rjyc->rijc/dot_general | solution.py:52
  55.2 7.5 %bitcast_dynamic-update-slice_fusion.2 = bf16[4,32,7,7,256]{4,2,3,1,0:T(8,128)(2,1)} fusion(bf16[4,32,7,7,256]{4,2,3,1,0:T(8,128)(2,1)} %get-tuple-element.230, s32[]{:T(128)} %get-tuple-element.229, f32[32,7,24,256]{3,0,2,1:T(8,128)S(1)} %fusion.66, f32[4,32,7,24]{3,2,1,0:T(8,128)S(1)} %get-tuple-element.237), kind=kOutput, calls=%fused_computation.2.clone.1 | convolution fusion | flops 115605504 | bytes 7472128 | tf_op jit(solution)/shard_map/while/body/eval_jaxpr/riy,rjyc->rijc/dot_general | solution.py:52
  62.6 5.1 %copy.77 = bf16[4,32,7,7,256]{4,3,2,1,0:T(8,128)(2,1)} copy(bf16[4,32,7,7,256]{4,2,3,1,0:T(8,128)(2,1)} %get-tuple-element.57) | data formatting | bytes 6422528 | tf_op jit(solution)/shard_map/convert_element_type | solution.py:107
  67.8 5.6 %convert_element_type.132 = bf16[128,12544]{1,0:T(8,128)(2,1)S(1)} reshape(bf16[4,32,7,7,256]{4,3,2,1,0:T(8,128)(2,1)} %copy.77) | data formatting | bytes 6422528 | tf_op jit(solution)/shard_map/convert_element_type | solution.py:107
  73.4 3.8 %fusion.39 = f32[128,256]{1,0:T(8,128)S(1)} fusion(bf16[128,12544]{1,0:T(8,128)(2,1)S(1)} %convert_element_type.132, bf16[12544,256]{1,0:T(8,128)(2,1)} %param.14), kind=kOutput, calls=%fused_computation.69 | convolution fusion | flops 822083584 | bytes 9764864 | tf_op jit(solution)/shard_map/dot_general | solution.py:108
  79.0 22.9 %all-reduce.2.cloned.1.call-done = bf16[128,512]{1,0:T(8,128)(2,1)} async-done(((bf16[128,512]{1,0:T(8,128)(2,1)}), bf16[128,512]{1,0:T(8,128)(2,1)}) %all-reduce.2.cloned.1.call-update) | async-done | bytes 131088 | tf_op jit(solution)/shard_map/psum | solution.py:110
  104.9 6.8 %convolution_convert_fusion = bf16[128,12544]{1,0:T(8,128)(2,1)} fusion(bf16[128,256]{1,0:T(8,128)(2,1)S(1)} %fusion.37, bf16[12544,256]{1,0:T(8,128)(2,1)} %param.14), kind=kOutput, calls=%fused_computation.21 | convolution fusion | flops 823689216 | bytes 9699328 | tf_op jit(solution)/shard_map/dot_general | solution.py:132
  111.7 9.3 %convert_element_type.129 = bf16[128,16,784]{2,1,0:T(8,128)(2,1)} reshape(bf16[4,32,7,7,256]{4,3,2,1,0:T(8,128)(2,1)} %copy.77) | data formatting | bytes 6422528 | tf_op jit(solution)/shard_map/convert_element_type | solution.py:107
  121.0 6.2 %copy.78 = bf16[128,16,784]{0,2,1:T(8,128)(2,1)} copy(bf16[128,16,784]{2,1,0:T(8,128)(2,1)} %convert_element_type.129) | data formatting | bytes 6422528 | tf_op jit(solution)/shard_map/convert_element_type | solution.py:107
  127.3 5.8 %all-to-all-start = ((bf16[128,16,784]{0,2,1:T(8,128)(2,1)}), bf16[128,16,784]{0,2,1:T(8,128)(2,1)S(1)}, u32[]{:S(2)}, u32[]{:S(2)}) async-start(bf16[128,16,784]{0,2,1:T(8,128)(2,1)} %copy.78), calls=%async_computation | async-start | bytes 6422528 | tf_op jit(solution)/shard_map/all_to_all | solution.py:127
  133.8 22.2 %reduce-scatter.2.cloned.1.call-done = bf16[64,12544]{1,0:T(8,128)(2,1)} async-done(((bf16[128,12544]{1,0:T(8,128)(2,1)}), bf16[64,12544]{1,0:T(8,128)(2,1)}) %reduce-scatter.2.cloned.1.call-update) | async-done | bytes 1605648 | tf_op jit(solution)/shard_map/reduce_scatter | solution.py:135
  160.9 21.7 %collective-permute-done.1 = f32[256,512]{1,0:T(8,128)S(1)} collective-permute-done((f32[256,512]{1,0:T(8,128)S(1)}, f32[256,512]{1,0:T(8,128)S(1)}, u32[]{:S(2)}, u32[]{:S(2)}) %collective-permute-start.1) | collective-permute-done | bytes 524320 | tf_op jit(solution)/shard_map/ppermute | solution.py:120
  184.1 24.8 %collective-permute-done.2 = f32[256,512]{1,0:T(8,128)S(1)} collective-permute-done((f32[256,512]{1,0:T(8,128)S(1)}, f32[256,512]{1,0:T(8,128)S(1)}, u32[]{:S(2)}, u32[]{:S(2)}) %collective-permute-start.2) | collective-permute-done | bytes 524320 | tf_op jit(solution)/shard_map/ppermute | solution.py:120
  209.7 5.8 %collective-permute-start.3 = (f32[256,512]{1,0:T(8,128)}, f32[256,512]{1,0:T(8,128)}, u32[]{:S(2)}, u32[]{:S(2)}) collective-permute-start(f32[256,512]{1,0:T(8,128)} %add.169), channel_id=1, source_target_pairs={{0,16},{2,18},{4,20},{6,22},{8,24},{10,26},{12,28},{14,30},{16,0},... | collective-permute-start | bytes 1572872 | tf_op jit(solution)/shard_map/ppermute | solution.py:120
  217.8 21.4 %collective-permute-done.3 = f32[256,512]{1,0:T(8,128)} collective-permute-done((f32[256,512]{1,0:T(8,128)}, f32[256,512]{1,0:T(8,128)}, u32[]{:S(2)}, u32[]{:S(2)}) %collective-permute-start.3) | collective-permute-done | bytes 524320 | tf_op jit(solution)/shard_map/ppermute | solution.py:120
  241.2 3.1 fusion.18
  244.3 17.0 %all-gather.6.cloned.1.call-done = bf16[128,12544]{1,0:T(8,128)(2,1)} async-done(((bf16[64,12544]{1,0:T(8,128)(2,1)}), bf16[128,12544]{1,0:T(8,128)(2,1)}) %all-gather.6.cloned.1.call-update) | async-done | bytes 3211280 | tf_op jit(solution)/shard_map/all_gather | solution.py:138
  261.3 5.1 %convert.3 = f32[4,32,12544]{2,1,0:T(8,128)} convert(bf16[4,32,12544]{2,1,0:T(8,128)(2,1)} %bitcast.115) | non-fusion elementwise | flops 1605632 | bytes 9633792 | tf_op jit(solution)/shard_map/reshape | solution.py:86
  266.5 51.9 %while.22 = (s32[]{:T(128)}, f32[84,3072]{1,0:T(8,128)}, bf16[4,32,7,84]{3,2,1,0:T(8,128)(2,1)}, f32[4,32,12544]{2,1,0:T(8,128)}, f32[4,32,7,12]{3,2,1,0:T(8,128)}, /*index=5*/s32[]{:T(128)}, s32[]{:T(128)}) while((s32[]{:T(128)}, f32[84,3072]{1,0:T(8,128)}, bf16[4,32,7,84]{3,2,1,0:T(8,128)(2,1)}, f32[4,32,12544]{2,1,0:T(8,128)}, ...), condition=%wide.region_8.9_spmd.clone, body=%wide.region_7.8_spmd.clone.sunk | while | flops 751951872 | bytes 21422432 | solution.py:88
  268.4 4.5 %fusion.71 = f32[32,7,256,12]{2,3,1,0:T(8,128)S(1)} fusion(f32[32,7,7,256]{3,2,1,0:T(8,128)S(1)} %reshape.239, f32[4,32,7,12]{3,2,1,0:T(8,128)} %get-tuple-element.259, s32[]{:T(128)} %get-tuple-element.248), kind=kOutput, calls=%fused_computation.14.clone.1 | convolution fusion | flops 57802752 | bytes 4489728 | tf_op jit(solution)/shard_map/while/body/eval_jaxpr/riy,rijc->rjyc/dot_general | solution.py:72
  272.9 2.4 copy.120
  280.5 4.5 %fusion.71 = f32[32,7,256,12]{2,3,1,0:T(8,128)S(1)} fusion(f32[32,7,7,256]{3,2,1,0:T(8,128)S(1)} %reshape.239, f32[4,32,7,12]{3,2,1,0:T(8,128)} %get-tuple-element.259, s32[]{:T(128)} %get-tuple-element.248), kind=kOutput, calls=%fused_computation.14.clone.1 | convolution fusion | flops 57802752 | bytes 4489728 | tf_op jit(solution)/shard_map/while/body/eval_jaxpr/riy,rijc->rjyc/dot_general | solution.py:72
  285.0 2.4 copy.120
  288.3 3.5 %convolution_add_fusion.2 = f32[84,3072]{1,0:T(8,128)} fusion(bf16[224,84]{1,0:T(8,128)(2,1)S(1)} %reshape.238, f32[224,3072]{1,0:T(8,128)S(1)} %bitcast.108, f32[84,3072]{1,0:T(8,128)} %get-tuple-element.249, pred[]{:T(512)S(6)} %compare.3), kind=kOutput, calls=%fused_computation.13.clone.1 | convolution fusion | flops 694149120 | bytes 4854529 | tf_op jit(solution)/shard_map/while/body/eval_jaxpr/dot_general | solution.py:73
  293.8 4.5 %fusion.71 = f32[32,7,256,12]{2,3,1,0:T(8,128)S(1)} fusion(f32[32,7,7,256]{3,2,1,0:T(8,128)S(1)} %reshape.239, f32[4,32,7,12]{3,2,1,0:T(8,128)} %get-tuple-element.259, s32[]{:T(128)} %get-tuple-element.248), kind=kOutput, calls=%fused_computation.14.clone.1 | convolution fusion | flops 57802752 | bytes 4489728 | tf_op jit(solution)/shard_map/while/body/eval_jaxpr/riy,rijc->rjyc/dot_general | solution.py:72
  301.6 3.5 %convolution_add_fusion.2 = f32[84,3072]{1,0:T(8,128)} fusion(bf16[224,84]{1,0:T(8,128)(2,1)S(1)} %reshape.238, f32[224,3072]{1,0:T(8,128)S(1)} %bitcast.108, f32[84,3072]{1,0:T(8,128)} %get-tuple-element.249, pred[]{:T(512)S(6)} %compare.3), kind=kOutput, calls=%fused_computation.13.clone.1 | convolution fusion | flops 694149120 | bytes 4854529 | tf_op jit(solution)/shard_map/while/body/eval_jaxpr/dot_general | solution.py:73
  307.1 4.5 %fusion.71 = f32[32,7,256,12]{2,3,1,0:T(8,128)S(1)} fusion(f32[32,7,7,256]{3,2,1,0:T(8,128)S(1)} %reshape.239, f32[4,32,7,12]{3,2,1,0:T(8,128)} %get-tuple-element.259, s32[]{:T(128)} %get-tuple-element.248), kind=kOutput, calls=%fused_computation.14.clone.1 | convolution fusion | flops 57802752 | bytes 4489728 | tf_op jit(solution)/shard_map/while/body/eval_jaxpr/riy,rijc->rjyc/dot_general | solution.py:72
  314.9 3.5 %convolution_add_fusion.2 = f32[84,3072]{1,0:T(8,128)} fusion(bf16[224,84]{1,0:T(8,128)(2,1)S(1)} %reshape.238, f32[224,3072]{1,0:T(8,128)S(1)} %bitcast.108, f32[84,3072]{1,0:T(8,128)} %get-tuple-element.249, pred[]{:T(512)S(6)} %compare.3), kind=kOutput, calls=%fused_computation.13.clone.1 | convolution fusion | flops 694149120 | bytes 4854529 | tf_op jit(solution)/shard_map/while/body/eval_jaxpr/dot_general | solution.py:73
  (94 shorter events, 48.4 us)
Async XLA Ops:
  7.2 70.7 %copy-start = (bf16[256,512]{1,0:T(8,128)(2,1)S(1)}, bf16[256,512]{1,0:T(8,128)(2,1)}, u32[]{:S(2)}) copy-start(bf16[256,512]{1,0:T(8,128)(2,1)} %param.15) | copy-start | bytes 786436
  7.2 94.7 %all-reduce.2.cloned.1.call-start = ((), (), s32[]{:S(2)}) async-start(), calls=%async_computation.2 | async-start | bytes 262144 | tf_op jit(solution)/shard_map/psum | solution.py:110
  10.7 17.0 %copy-start.2 = (bf16[128,7,84]{0,2,1:T(8,128)(2,1)}, bf16[128,7,84]{0,2,1:T(8,128)(2,1)S(1)}, u32[]{:S(2)}) copy-start(bf16[128,7,84]{0,2,1:T(8,128)(2,1)S(1)} %multiply_convert_fusion) | copy-start | bytes 451588
  77.2 0.7 copy-start.4
  78.8 77.3 %reduce-scatter.2.cloned.1.call-start = ((), (), s32[]{:S(2)}) async-start(), calls=%async_computation.4 | async-start | bytes 4816896 | tf_op jit(solution)/shard_map/reduce_scatter | solution.py:135
  103.1 0.7 copy-start.6
  104.9 6.8 %copy-start.7 = (bf16[128,256]{1,0:T(8,128)(2,1)}, bf16[128,256]{1,0:T(8,128)(2,1)S(1)}, u32[]{:S(2)}) copy-start(bf16[128,256]{1,0:T(8,128)(2,1)S(1)} %fusion.37) | copy-start | bytes 196612
  127.3 28.8 %copy-start.5 = (f32[128,256]{1,0:T(8,128)S(1)}, f32[128,256]{1,0:T(8,128)}, u32[]{:S(2)}) copy-start(f32[128,256]{1,0:T(8,128)} %copy-done.4) | copy-start | bytes 393220
  127.3 114.0 %all-to-all-start = ((bf16[128,16,784]{0,2,1:T(8,128)(2,1)}), bf16[128,16,784]{0,2,1:T(8,128)(2,1)S(1)}, u32[]{:S(2)}, u32[]{:S(2)}) async-start(bf16[128,16,784]{0,2,1:T(8,128)(2,1)} %copy.78), calls=%async_computation | async-start | bytes 6422528 | tf_op jit(solution)/shard_map/all_to_all | solution.py:127
  133.0 108.2 %all-gather.4.cloned.1.call-start = ((), (), s32[]{:S(2)}) async-start(), calls=%async_computation.3 | async-start | bytes 1114112 | tf_op jit(solution)/shard_map/all_gather | solution.py:128
  133.8 127.6 %all-gather.6.cloned.1.call-start = ((), (), s32[]{:S(2)}) async-start(), calls=%async_computation.5 | async-start | bytes 4816896 | tf_op jit(solution)/shard_map/all_gather | solution.py:138
  156.0 59.5 %copy-start.3 = (bf16[128,7,84]{0,2,1:T(8,128)(2,1)S(1)}, bf16[128,7,84]{0,2,1:T(8,128)(2,1)}, u32[]{:S(2)}) copy-start(bf16[128,7,84]{0,2,1:T(8,128)(2,1)} %copy-done.2) | copy-start | bytes 451588
  157.3 2.0 collective-permute-start
  159.3 23.2 %collective-permute-start.1 = (f32[256,512]{1,0:T(8,128)S(1)}, f32[256,512]{1,0:T(8,128)S(1)}, u32[]{:S(2)}, u32[]{:S(2)}) collective-permute-start(f32[256,512]{1,0:T(8,128)S(1)} %add.167), channel_id=1, source_target_pairs={{0,4},{2,6},{4,0},{6,2},{8,12},{10,14},{12,8},{14,10},{16,20},{18,... | collective-permute-start | bytes 1572872 | tf_op jit(solution)/shard_map/ppermute | solution.py:120
  182.6 26.2 %collective-permute-start.2 = (f32[256,512]{1,0:T(8,128)S(1)}, f32[256,512]{1,0:T(8,128)S(1)}, u32[]{:S(2)}, u32[]{:S(2)}) collective-permute-start(f32[256,512]{1,0:T(8,128)S(1)} %add.168), channel_id=1, source_target_pairs={{0,8},{2,10},{4,12},{6,14},{8,0},{10,2},{12,4},{14,6},{16,24},{18,... | collective-permute-start | bytes 1572872 | tf_op jit(solution)/shard_map/ppermute | solution.py:120
  209.7 29.4 %collective-permute-start.3 = (f32[256,512]{1,0:T(8,128)}, f32[256,512]{1,0:T(8,128)}, u32[]{:S(2)}, u32[]{:S(2)}) collective-permute-start(f32[256,512]{1,0:T(8,128)} %add.169), channel_id=1, source_target_pairs={{0,16},{2,18},{4,20},{6,22},{8,24},{10,26},{12,28},{14,30},{16,0},... | collective-permute-start | bytes 1572872 | tf_op jit(solution)/shard_map/ppermute | solution.py:120
  318.4 3.6 %copy-start.1 = (bf16[256,512]{1,0:T(8,128)(2,1)S(1)}, bf16[256,512]{1,0:T(8,128)(2,1)}, u32[]{:S(2)}) copy-start(bf16[256,512]{1,0:T(8,128)(2,1)} %param.15) | copy-start | bytes 786436
Sparse Core Ops, SparseCore 0:
  78.9 22.9 all-reduce.1
  111.9 44.1 reduce-scatter.1
  158.2 54.5 all-gather.3
  214.2 47.1 all-gather.5
